TPU v7x, 32 devices: a whole 2x2x4 slice. The times are simulated.
32 devices in a mesh: gx: 4 (over y, x), gy: 2 (over core), gz: 4 (over z).
Axes of the slice: x: 2, y: 2, z: 4, core: 2. Of those that a mesh axis runs over, the one named last changes fastest.
Arguments:
- conserved: float32 [5, 64, 32, 512], P(None, 'gx', 'gy', 'gz'), as said below
Outputs:
- advanced: float32 [5, 64, 32, 512], P(None, 'gx', 'gy', 'gz')
Inputs may be any that keep to these rules, and one draw needn't show every extreme that they name: `conserved`: every cell has positive density and positive pressure (energy above the kinetic energy).
All inputs are finite; a program needn't handle non-finite values. Where the computation divides by a largest or mean magnitude, that divisor is 1e-20 or more.
Results may differ from a plain program's by a relative error of at most 0.000066.
Values sent between devices are 32-bit elements; how exact they have to be, the bound alone decides.
A program may use at most 64 MiB of HBM per device.

v0:
```python
import jax
import jax.numpy as jnp
from jax import lax
from jax.sharding import PartitionSpec as P

gamma_gas = 1.4
weno_eps = 1e-06
courant = 0.4


def padded(shard, sides, width):
    for axis, dim in sides:
        devices, length = (lax.axis_size(axis), shard.shape[dim])
        up = [(i, (i + 1) % devices) for i in range(devices)]
        down = [(j, i) for i, j in up]
        last = lax.slice_in_dim(shard, length - width, length, axis=dim)
        first = lax.slice_in_dim(shard, 0, width, axis=dim)
        before = lax.ppermute(last, axis, up)
        after = lax.ppermute(first, axis, down)
        shard = jnp.concatenate([before, shard, after], axis=dim)
    return shard


def primitives(components):
    density = components[0]
    vel_normal = components[1] / density
    vel_first = components[2] / density
    vel_second = components[3] / density
    kinetic = 0.5 * (vel_normal * vel_normal + vel_first * vel_first + vel_second * vel_second)
    pressure = (gamma_gas - 1.0) * (components[4] - density * kinetic)
    return (density, vel_normal, vel_first, vel_second, kinetic, pressure)


def multiply_rows(matrix, vector):
    result = []
    for matrix_row in matrix:
        accum = None
        for coefficient, component in zip(matrix_row, vector):
            if coefficient is None:
                continue
            product_term = component * coefficient
            accum = product_term if accum is None else accum + product_term
        result.append(accum)
    return result


def weno_face(far_left, near_left, centre, near_right, far_right):
    poly_left = (2.0 * far_left - 7.0 * near_left + 11.0 * centre) / 6.0
    poly_mid = (-near_left + 5.0 * centre + 2.0 * near_right) / 6.0
    poly_right = (2.0 * centre + 5.0 * near_right - far_right) / 6.0
    diff_one = far_left - 2.0 * near_left + centre
    diff_two = far_left - 4.0 * near_left + 3.0 * centre
    smooth_left = 13.0 / 12.0 * diff_one * diff_one + 0.25 * diff_two * diff_two
    diff_one = near_left - 2.0 * centre + near_right
    diff_two = near_left - near_right
    smooth_mid = 13.0 / 12.0 * diff_one * diff_one + 0.25 * diff_two * diff_two
    diff_one = centre - 2.0 * near_right + far_right
    diff_two = 3.0 * centre - 4.0 * near_right + far_right
    smooth_right = 13.0 / 12.0 * diff_one * diff_one + 0.25 * diff_two * diff_two
    weight_left = 0.1 / ((weno_eps + smooth_left) * (weno_eps + smooth_left))
    weight_mid = 0.6 / ((weno_eps + smooth_mid) * (weno_eps + smooth_mid))
    weight_right = 0.3 / ((weno_eps + smooth_right) * (weno_eps + smooth_right))
    return (weight_left * poly_left + weight_mid * poly_mid + weight_right * poly_right) / (
        weight_left + weight_mid + weight_right
    )


def face_divergence(components, line_axis, wave_speed, cell_count):
    length = components[0].shape[line_axis] - 6
    face_count = length + 1

    def window(array_item, start, count):
        return lax.slice_in_dim(array_item, start, start + count, axis=line_axis)

    density, vel_normal, vel_first, vel_second, kinetic, pressure = primitives(components)
    fluxes = [
        components[1],
        components[1] * vel_normal + pressure,
        components[2] * vel_normal,
        components[3] * vel_normal,
        (components[4] + pressure) * vel_normal,
    ]
    split_plus = [
        0.5 * (flux + wave_speed * component) for flux, component in zip(fluxes, components)
    ]
    split_minus = [
        0.5 * (flux - wave_speed * component) for flux, component in zip(fluxes, components)
    ]
    face_mean = [
        0.5 * (window(component, 2, face_count) + window(component, 3, face_count))
        for component in components
    ]
    mean_density, mean_normal, mean_first, mean_second, mean_kinetic, mean_pressure = primitives(
        face_mean
    )
    enthalpy = (face_mean[4] + mean_pressure) / mean_density
    sound_speed = jnp.sqrt(gamma_gas * mean_pressure / mean_density)
    inv_sound = 1.0 / sound_speed
    coef_one = (gamma_gas - 1.0) / (sound_speed * sound_speed)
    coef_two = coef_one * mean_kinetic
    left_rows = [
        [
            0.5 * (coef_two + mean_normal * inv_sound),
            -0.5 * (coef_one * mean_normal + inv_sound),
            -0.5 * coef_one * mean_first,
            -0.5 * coef_one * mean_second,
            0.5 * coef_one,
        ],
        [-mean_first, None, 1.0, None, None],
        [-mean_second, None, None, 1.0, None],
        [
            1.0 - coef_two,
            coef_one * mean_normal,
            coef_one * mean_first,
            coef_one * mean_second,
            -coef_one,
        ],
        [
            0.5 * (coef_two - mean_normal * inv_sound),
            -0.5 * (coef_one * mean_normal - inv_sound),
            -0.5 * coef_one * mean_first,
            -0.5 * coef_one * mean_second,
            0.5 * coef_one,
        ],
    ]
    right_cols = [
        [1.0, None, None, 1.0, 1.0],
        [mean_normal - sound_speed, None, None, mean_normal, mean_normal + sound_speed],
        [mean_first, 1.0, None, mean_first, mean_first],
        [mean_second, None, 1.0, mean_second, mean_second],
        [
            enthalpy - mean_normal * sound_speed,
            mean_first,
            mean_second,
            mean_kinetic,
            enthalpy + mean_normal * sound_speed,
        ],
    ]
    positive = [
        multiply_rows(
            left_rows, [window(component, offset, face_count) for component in split_plus]
        )
        for offset in range(5)
    ]
    negative = [
        multiply_rows(
            left_rows, [window(component, offset, face_count) for component in split_minus]
        )
        for offset in range(1, 6)
    ]
    wave_sums = []
    for wave_index in range(5):
        upwind = weno_face(*[positive[offset][wave_index] for offset in range(5)])
        downwind = weno_face(*[negative[offset][wave_index] for offset in (4, 3, 2, 1, 0)])
        wave_sums.append(upwind + downwind)
    face_flux = multiply_rows(right_cols, wave_sums)
    return [-(window(flux, 1, length) - window(flux, 0, length)) * cell_count for flux in face_flux]


def component_order(direction):
    if direction == 0:
        return [0, 1, 2, 3, 4]
    if direction == 1:
        return [0, 2, 1, 3, 4]
    return [0, 3, 1, 2, 4]


def direction_terms(padded_slab, line_axis, direction, wave_speed, cell_count):
    comp_order = component_order(direction)
    result = face_divergence(
        [padded_slab[index] for index in comp_order], line_axis, wave_speed, cell_count
    )
    placed = [None] * 5
    for index, target in enumerate(comp_order):
        placed[target] = result[index]
    return jnp.stack(placed)


def per_device(conserved):
    cells_x = conserved.shape[1] * lax.axis_size("gx")
    cells_y = conserved.shape[2] * lax.axis_size("gy")
    cells_z = conserved.shape[3] * lax.axis_size("gz")
    components = [conserved[index] for index in range(5)]
    density, vel_one, vel_two, vel_three, kinetic, pressure = primitives(components)
    sound_speed = jnp.sqrt(gamma_gas * pressure / density)
    local_x = jnp.max(jnp.abs(vel_one) + sound_speed)
    local_y = jnp.max(jnp.abs(vel_two) + sound_speed)
    local_z = jnp.max(jnp.abs(vel_three) + sound_speed)
    speed_x, speed_y, speed_z = lax.pmax((local_x, local_y, local_z), ("gx", "gy", "gz"))
    step = courant / (speed_x * cells_x + speed_y * cells_y + speed_z * cells_z)
    along_x = padded(conserved, (("gx", 1),), 3)
    tendency = direction_terms(along_x, 0, 0, speed_x, cells_x)
    along_y = padded(conserved, (("gy", 2),), 3)
    tendency = tendency + direction_terms(along_y, 1, 1, speed_y, cells_y)
    along_z = padded(conserved, (("gz", 3),), 3)
    tendency = tendency + direction_terms(along_z, 2, 2, speed_z, cells_z)
    return conserved + step * tendency


def solution(mesh):
    return jax.shard_map(
        per_device,
        mesh=mesh,
        in_specs=(P(None, "gx", "gy", "gz"),),
        out_specs=P(None, "gx", "gy", "gz"),
        check_vma=False,
    )
```

profile of v0, /device:TPU:0, one launch (start us, length us, event | category | flops | bytes accessed | tf_op | source)
XLA Modules:
  0.0 101.0 jit_solution(7025035947713160962)
XLA Ops:
  0.0 1.5 %fusion.481 = (f32[5,16,16,3]{3,2,1,0:T(8,128)S(1)}, f32[5,16,16,3]{3,2,1,0:T(8,128)S(1)}) fusion(f32[5,16,16,128]{3,2,1,0:T(8,128)} %param.1), kind=kLoop, calls=%fused_computation.899 | loop fusion | bytes 61440 | tf_op jit(solution)/shard_map/slice | solution.py:16
  1.5 0.0 copy-start
  1.5 0.6 copy.22
  2.1 5.1 %collective-permute-start.5 = (f32[5,16,16,3]{2,1,3,0:T(8,128)S(1)}, f32[5,16,16,3]{2,1,3,0:T(8,128)S(1)}, u32[]{:S(2)}, u32[]{:S(2)}) collective-permute-start(f32[5,16,16,3]{2,1,3,0:T(8,128)S(1)} %copy.22), channel_id=1, source_target_pairs={{1,0},{2,1},{3,2},{0,3},{5,4},{6,5},{7,6},{4,7},{9,8},{10,9},{11,1... | collective-permute-start | bytes 46088 | tf_op jit(solution)/shard_map/ppermute | solution.py:19
  7.2 0.6 copy.21
  7.8 0.1 collective-permute-start.4
  7.9 0.0 copy-done
  7.9 0.2 copy.19
  8.1 0.7 fusion.479
  8.8 0.0 collective-permute-start.2
  8.8 0.5 collective-permute-start.3
  9.3 0.1 fusion.480
  9.4 2.5 %collective-permute-start.1 = (f32[5,3,16,128]{3,1,2,0:T(4,128)S(1)}, f32[5,3,16,128]{3,1,2,0:T(4,128)S(1)}, u32[]{:S(2)}, u32[]{:S(2)}) collective-permute-start(f32[5,3,16,128]{3,1,2,0:T(4,128)S(1)} %get-tuple-element.100), channel_id=1, source_target_pairs={{8,0},{16,8},{24,16},{0,24},{9,1},{17,9},{25,17},{1,25},{10,2},{18... | collective-permute-start | bytes 368648 | tf_op jit(solution)/shard_map/ppermute | solution.py:19
  11.9 0.8 add_reduce_fusion.1
  12.7 39.4 %all-reduce = (f32[]{:T(128)}, f32[]{:T(128)}, f32[]{:T(128)}) all-reduce(f32[]{:T(128)} %get-tuple-element.6, f32[]{:T(128)} %get-tuple-element.7, f32[]{:T(128)} %get-tuple-element.5), channel_id=1, replica_groups=mesh['gx'=4,'gy'=2,'gz'=4] {'gx','gy','gz'}, use_global_device_ids=true, to_apply=%region_5.0 | all-reduce | flops 3 | bytes 24 | tf_op jit(solution)/shard_map/pmax | solution.py:189
  54.0 0.0 collective-permute-done.5
  54.0 2.3 %collective-permute-start = (f32[5,3,16,128]{3,1,2,0:T(4,128)S(1)}, f32[5,3,16,128]{3,1,2,0:T(4,128)S(1)}, u32[]{:S(2)}, u32[]{:S(2)}) collective-permute-start(f32[5,3,16,128]{3,1,2,0:T(4,128)S(1)} %get-tuple-element.99), channel_id=1, source_target_pairs={{0,8},{8,16},{16,24},{24,0},{1,9},{9,17},{17,25},{25,1},{2,10},{10... | collective-permute-start | bytes 368648 | tf_op jit(solution)/shard_map/ppermute | solution.py:18
  56.3 0.6 copy.18
  56.9 0.0 collective-permute-done.4
  56.9 1.4 %copy.16 = f32[5,16,16,3]{3,1,2,0:T(8,128)S(1)} copy(f32[5,16,16,3]{2,1,3,0:T(8,128)} %collective-permute-done.4) | data formatting | bytes 30720 | tf_op jit(solution)/shard_map/ppermute | solution.py:18
  58.3 0.6 pad_maximum_fusion
  58.9 0.1 slice_bitcast_fusion.4
  59.0 0.9 subtract_multiply_fusion
  59.9 1.1 %add_multiply_fusion.4 = (f32[16,16,134]{2,0,1:T(8,128)S(1)}, f32[16,16,134]{2,0,1:T(8,128)S(1)}, f32[16,16,134]{2,0,1:T(8,128)S(1)}, f32[16,16,134]{2,0,1:T(8,1...) fusion(f32[]{:T(128)} %get-tuple-element.8, ...), kind=kLoop, calls=%fused_computation.288 | loop fusion | flops 994816 | bytes 2195460 | tf_op jit(solution)/shard_map/mul | solution.py:84
  61.0 17.0 %multiply_add_fusion.1 = (f32[16,16,129]{2,0,1:T(8,128)S(1)}, f32[16,16,129]{2,0,1:T(8,128)S(1)}, f32[16,16,129]{2,0,1:T(8,128)S(1)}, f32[16,16,129]{2,0,1:T(8,1...) fusion(f32[16,16,134]{2,0,1:T(8,128)S(1)} %get-tuple-element.64, ...), kind=kLoop, calls=%fused_computation.269 | loop fusion | flops 32594688 | bytes 9246720 | tf_op jit(solution)/shard_map/add | solution.py:42
  78.0 0.3 multiply_add_fusion.2
  78.3 0.1 fusion.419
  78.4 0.1 fusion.415
  78.5 0.1 fusion.411
  78.6 0.1 fusion.407
  78.7 0.0 collective-permute-done.2
  78.7 0.2 constant_dynamic-update-slice_fusion.3
  78.9 0.0 collective-permute-done.3
  79.0 0.1 slice_bitcast_fusion.13
  79.0 0.8 subtract_multiply_fusion.12
  79.8 0.9 add_multiply_fusion.18
  80.7 0.2 divide_sqrt_fusion.2
  80.9 6.5 %multiply_add_fusion.12 = (f32[16,17,128]{2,0,1:T(8,128)S(1)}, f32[16,17,128]{2,0,1:T(8,128)S(1)}, f32[16,17,128]{2,0,1:T(8,128)S(1)}, f32[16,17,128]{2,0,1:T(8,...) fusion(f32[16,17,128]{2,0,1:T(8,128)S(1)} %get-tuple-element.22, ...), kind=kLoop, calls=%fused_computation.749 | loop fusion | flops 33910784 | bytes 8773632 | tf_op jit(solution)/shard_map/add | solution.py:42
  87.4 0.1 multiply_add_fusion.13
  87.5 0.0 collective-permute-done.1
  87.5 0.0 collective-permute-done
  87.5 0.2 pad_maximum_fusion.1
  87.7 0.7 subtract_multiply_fusion.6
  88.4 0.8 add_multiply_fusion.11
  89.2 0.1 constant_dynamic-update-slice_fusion
  89.2 0.1 fusion.268
  89.3 0.1 fusion.265
  89.4 9.6 %multiply_add_fusion.6 = (f32[17,16,128]{2,0,1:T(8,128)S(1)}, f32[17,16,128]{2,0,1:T(8,128)S(1)}, f32[17,16,128]{2,0,1:T(8,128)S(1)}, f32[17,16,128]{2,0,1:T(8,1...) fusion(f32[17,16,128]{2,0,1:T(8,128)S(1)} %get-tuple-element.34, ...), kind=kLoop, calls=%fused_computation.536 | loop fusion | flops 34015232 | bytes 9412608 | tf_op jit(solution)/shard_map/add | solution.py:42
  99.0 0.3 multiply_add_fusion.7
  99.5 0.1 fusion.403
  99.6 0.4 multiply_add_fusion
  100.0 1.0 %copy.20 = f32[5,16,16,128]{3,2,1,0:T(8,128)} copy(f32[5,16,16,128]{3,1,2,0:T(8,128)S(1)} %multiply_add_fusion) | data formatting | bytes 1310720 | tf_op jit(solution)/shard_map/add | solution.py:197
  (11 shorter events, 0.2 us)
Async XLA Ops:
  1.5 6.3 %copy-start = (f32[5,16,16,128]{3,2,1,0:T(8,128)S(1)}, f32[5,16,16,128]{3,2,1,0:T(8,128)}, u32[]{:S(2)}) copy-start(f32[5,16,16,128]{3,2,1,0:T(8,128)} %param.1) | copy-start | bytes 1966084
  2.1 51.9 %collective-permute-start.5 = (f32[5,16,16,3]{2,1,3,0:T(8,128)S(1)}, f32[5,16,16,3]{2,1,3,0:T(8,128)S(1)}, u32[]{:S(2)}, u32[]{:S(2)}) collective-permute-start(f32[5,16,16,3]{2,1,3,0:T(8,128)S(1)} %copy.22), channel_id=1, source_target_pairs={{1,0},{2,1},{3,2},{0,3},{5,4},{6,5},{7,6},{4,7},{9,8},{10,9},{11,1... | collective-permute-start | bytes 46088 | tf_op jit(solution)/shard_map/ppermute | solution.py:19
  7.8 49.1 %collective-permute-start.4 = (f32[5,16,16,3]{2,1,3,0:T(8,128)S(1)}, f32[5,16,16,3]{2,1,3,0:T(8,128)}, u32[]{:S(2)}, u32[]{:S(2)}) collective-permute-start(f32[5,16,16,3]{2,1,3,0:T(8,128)S(1)} %copy.21), channel_id=1, source_target_pairs={{0,1},{1,2},{2,3},{3,0},{4,5},{5,6},{6,7},{7,4},{8,9},{9,10},{10,1... | collective-permute-start | bytes 46088 | tf_op jit(solution)/shard_map/ppermute | solution.py:18
  8.8 69.9 %collective-permute-start.2 = (f32[5,16,3,128]{3,1,2,0:T(8,128)}, f32[5,16,3,128]{3,1,2,0:T(8,128)S(1)}, u32[]{:S(2)}, u32[]{:S(2)}) collective-permute-start(f32[5,16,3,128]{3,1,2,0:T(8,128)} %get-tuple-element.96), channel_id=1, source_target_pairs={{0,4},{4,0},{1,5},{5,1},{2,6},{6,2},{3,7},{7,3},{8,12},{12,8},{9,1... | collective-permute-start | bytes 368648 | tf_op jit(solution)/shard_map/ppermute | solution.py:18
  8.8 70.1 %collective-permute-start.3 = (f32[5,16,3,128]{3,1,2,0:T(8,128)}, f32[5,16,3,128]{3,1,2,0:T(8,128)S(1)}, u32[]{:S(2)}, u32[]{:S(2)}) collective-permute-start(f32[5,16,3,128]{3,1,2,0:T(8,128)} %get-tuple-element.95), channel_id=1, source_target_pairs={{4,0},{0,4},{5,1},{1,5},{6,2},{2,6},{7,3},{3,7},{12,8},{8,12},{13,... | collective-permute-start | bytes 368648 | tf_op jit(solution)/shard_map/ppermute | solution.py:19
  9.4 78.2 %collective-permute-start.1 = (f32[5,3,16,128]{3,1,2,0:T(4,128)S(1)}, f32[5,3,16,128]{3,1,2,0:T(4,128)S(1)}, u32[]{:S(2)}, u32[]{:S(2)}) collective-permute-start(f32[5,3,16,128]{3,1,2,0:T(4,128)S(1)} %get-tuple-element.100), channel_id=1, source_target_pairs={{8,0},{16,8},{24,16},{0,24},{9,1},{17,9},{25,17},{1,25},{10,2},{18... | collective-permute-start | bytes 368648 | tf_op jit(solution)/shard_map/ppermute | solution.py:19
  54.0 33.5 %collective-permute-start = (f32[5,3,16,128]{3,1,2,0:T(4,128)S(1)}, f32[5,3,16,128]{3,1,2,0:T(4,128)S(1)}, u32[]{:S(2)}, u32[]{:S(2)}) collective-permute-start(f32[5,3,16,128]{3,1,2,0:T(4,128)S(1)} %get-tuple-element.99), channel_id=1, source_target_pairs={{0,8},{8,16},{16,24},{24,0},{1,9},{9,17},{17,25},{25,1},{2,10},{10... | collective-permute-start | bytes 368648 | tf_op jit(solution)/shard_map/ppermute | solution.py:18
where the time goes:
time: 101 us
  other arithmetic  41.7 us (41%)
  blocking collectives  39.4 us (39%)
  starting transfers between devices  10.5 us (10%)
  local copies, waits for them, and re-layouts  7.14 us (7%)
  between operations  2.3 us (2%)
    pmax x1, blocking collectives, per_device(): lax.pmax((local_x, local_y, local_z), ('gx', 'gy', 'gz'))  39.4 us
    add x6, other arithmetic, multiply_rows(): accum = product_term if accum is None else accum + product_term  33.7 us
    ppermute x3, starting transfers between devices, padded(): after = lax.ppermute(first, axis, down)  8.13 us
    mul x3, other arithmetic, face_divergence(): 0.5 * (flux + wave_speed * component)  2.74 us
    ppermute x3, starting transfers between devices, padded(): before = lax.ppermute(last, axis, up)  2.38 us
    mul x3, other arithmetic, face_divergence(): 0.5 * (flux - wave_speed * component)  2.33 us
  transfers between devices with their start and end apart: 6, of which 0 were waited for; matrix products, arithmetic and copies ran while one was open for 33% of the time, Pallas kernels for 0%

commit v1 on v0

v1 whole, which is shorter than its diff:
```python
import functools

import jax
import jax.numpy as jnp
from jax import lax
from jax.experimental import pallas as pl
from jax.experimental.pallas import tpu as pltpu
from jax.sharding import PartitionSpec as P

GAMMA = 1.4
EPS = 1e-06
COURANT = 0.4
K13 = 13.0 / 3.0
MESH = pl.DeviceIdType.MESH
AXES = ("gx", "gy", "gz")
ORDERS = ([0, 1, 2, 3, 4], [0, 2, 1, 3, 4], [0, 3, 1, 2, 4])
LANES = 128


def exchange_kernel(
    sizes, shape, cons, xh, yh, zh, zt, top, ysend, zsend, mine, theirs,
    halo_send, halo_recv, max_send, max_recv,
):
    lx, ly, lz = shape
    rows = lx * ly
    groups = rows // LANES
    blocks = 8 // groups
    inner = lz // blocks
    peers = []
    for axis, size in zip(AXES, sizes):
        me = lax.axis_index(axis)
        peers.append([{axis: lax.rem(me + k, size)} for k in range(1, size)])
    barrier = pltpu.get_barrier_semaphore()
    count = 0
    for axis_peers in peers:
        for peer in axis_peers:
            pl.semaphore_signal(barrier, inc=1, device_id=peer, device_id_type=MESH)
            count += 1

    best = [None] * 3
    for j in range(rows // 8):
        q = [cons[c, pl.ds(8 * j, 8), :] for c in range(5)]
        inv = 1.0 / q[0]
        vel = [q[d] * inv for d in (1, 2, 3)]
        kinetic = 0.5 * (vel[0] * vel[0] + vel[1] * vel[1] + vel[2] * vel[2])
        sound = jnp.sqrt((GAMMA * (GAMMA - 1.0)) * (q[4] * inv - kinetic))
        for d in range(3):
            value = jnp.abs(vel[d]) + sound
            best[d] = value if best[d] is None else jnp.maximum(best[d], value)
    for d in range(3):
        mine[0, pl.ds(8 * d, 8), :] = best[d]

    for c in range(5):
        for k in range(3):
            ysend[0, c, pl.ds(k * lx, lx), :] = cons[c, pl.ds(ly - 3 + k, lx, stride=ly), :]
            ysend[1, c, pl.ds(k * lx, lx), :] = cons[c, pl.ds(k, lx, stride=ly), :]

    def halo(slot, src, dst, axis, size, up):
        me = lax.axis_index(axis)
        target = lax.rem(me + (1 if up else size - 1), size)
        return pltpu.make_async_remote_copy(
            src_ref=src, dst_ref=dst, send_sem=halo_send.at[slot], recv_sem=halo_recv.at[slot],
            device_id={axis: target}, device_id_type=MESH,
        )

    def spread(stage):
        axis, size = AXES[stage], sizes[stage]
        copies = []
        for k in range(size - 1):
            slot = sum(s - 1 for s in sizes[:stage]) + k
            copy = pltpu.make_async_remote_copy(
                src_ref=mine.at[position[stage]], dst_ref=theirs.at[slot],
                send_sem=max_send.at[slot], recv_sem=max_recv.at[slot],
                device_id=peers[stage][k], device_id_type=MESH,
            )
            copy.start()
            copies.append((slot, copy))
        return copies

    def gather(stage, copies):
        value = mine[position[stage]]
        for slot, copy in copies:
            copy.wait_recv()
            value = jnp.maximum(value, theirs[slot])
        return value

    order = (1, 2, 0)
    position = {stage: place for place, stage in enumerate(order)}
    started = []
    pl.semaphore_wait(barrier, count)
    copies = spread(order[0])
    started += copies
    edge = 3 * ly
    halos = [
        halo(0, cons.at[:, pl.ds(rows - edge, edge), :], xh.at[0], "gx", sizes[0], True),
        halo(1, cons.at[:, pl.ds(0, edge), :], xh.at[1], "gx", sizes[0], False),
        halo(2, ysend.at[0], yh.at[0], "gy", sizes[1], True),
        halo(3, ysend.at[1], yh.at[1], "gy", sizes[1], False),
    ]
    value = gather(order[0], copies)
    mine[1] = value
    copies = spread(order[1])
    started += copies
    for copy in halos:
        copy.start()

    for c in range(5):
        for g in range(groups):
            turned = jnp.transpose(cons[c, pl.ds(g * LANES, LANES), :])
            for b in range(blocks):
                zt[c, pl.ds(b * groups + g, inner, stride=8), :] = turned[b * inner:(b + 1) * inner]
                if b == blocks - 1:
                    for k in range(3):
                        zsend[0, c, k, g:g + 1, :] = turned[lz - 3 + k:lz - 2 + k]
                if b == 0:
                    for k in range(3):
                        zsend[1, c, k, g:g + 1, :] = turned[k:k + 1]

    value = gather(order[1], copies)
    mine[2] = value
    copies = spread(order[2])
    started += copies
    more = [
        halo(4, zsend.at[0], zh.at[0], "gz", sizes[2], True),
        halo(5, zsend.at[1], zh.at[1], "gz", sizes[2], False),
    ]
    for copy in more:
        copy.start()
    top[...] = gather(order[2], copies)
    for _, copy in started:
        copy.wait_send()
    for copy in halos + more:
        copy.wait()


def project(u, vn, va, vb, kin, b1h, ich):
    a = u[4] + kin * u[0] - vn * u[1] - va * u[2] - vb * u[3]
    a = b1h * a
    b = (vn * u[0] - u[1]) * ich
    return [a + b, u[2] - va * u[0], u[3] - vb * u[0], u[0] - (a + a), a - b]


def nonlinear(e1, e2, e3, f0, f1):
    f2 = e3 - (f1 + e2)
    q0 = 1.0 / ((K13 * (e1 * e1) + EPS) + f0 * f0)
    q1 = 1.0 / ((K13 * (e2 * e2) + EPS) + f1 * f1)
    q2 = 1.0 / ((K13 * (e3 * e3) + EPS) + f2 * f2)
    w0 = q0 * q0
    w2 = 3.0 * (q2 * q2)
    n0 = e1 - e2
    return (w0 * (n0 + n0) + w2 * (e2 - e3)) / (w0 + w2 + 6.0 * (q1 * q1))


def flux_sweep(direction, slots, lane_rows, quarter, q, p, m, f6, ep, em, hp, hm, flux):
    order = ORDERS[direction]

    def at(ref, c, j):
        return ref[c, pl.ds(pl.multiple_of(8 * j, 8), 8), :]

    def put(ref, c, j, value):
        ref[c, pl.ds(pl.multiple_of(8 * j, 8), 8), :] = value

    r = lane_rows

    def cell(j, _):
        s = [at(q, order[c], j) for c in range(5)]
        inv = 1.0 / s[0]
        vq = s[1] * (0.25 * inv)
        pq = 0.25 * (GAMMA - 1.0) * (s[4] - (0.5 * inv) * (s[1] * s[1] + s[2] * s[2] + s[3] * s[3]))
        f = [0.25 * s[1], s[1] * vq + pq, s[2] * vq, s[3] * vq, s[4] * vq + 4.0 * (pq * vq)]
        for c in range(5):
            sq = quarter * s[c]
            put(p, c, j, f[c] + sq)
            put(m, c, j, f[c] - sq)
            put(f6, c, j, 6.0 * f[c])
        return 0

    lax.fori_loop(0, (slots + 6) * r, cell, 0, unroll=2)

    def differ(i, _):
        j = i + r
        for c in range(5):
            for src, e, h in ((p, ep, hp), (m, em, hm)):
                low, mid, high = at(src, c, j - r), at(src, c, j), at(src, c, j + r)
                below = mid - low
                put(e, c, j, (high - mid) - below)
                put(h, c, j, below + below)
        return 0

    lax.fori_loop(0, (slots + 4) * r, differ, 0, unroll=2)

    def face(j, _):
        mean = [at(q, order[c], j + 2 * r) + at(q, order[c], j + 3 * r) for c in range(5)]
        inv = 1.0 / mean[0]
        vn, va, vb = mean[1] * inv, mean[2] * inv, mean[3] * inv
        kin = 0.5 * (vn * vn + va * va + vb * vb)
        c2 = GAMMA * (GAMMA - 1.0) * (mean[4] * inv - kin)
        ic = lax.rsqrt(c2)
        b1h = (0.5 * (GAMMA - 1.0)) * (ic * ic)
        ich = 0.5 * ic
        args = (vn, va, vb, kin, b1h, ich)
        e2p = [at(ep, c, j + 2 * r) for c in range(5)]
        e1, e3 = ([at(ep, c, j + k * r) for c in range(5)] for k in (1, 3))
        h = [at(hp, c, j + 2 * r) for c in range(5)]
        e1, e2, e3, h = (project(u, *args) for u in (e1, e2p, e3, h))
        n = [nonlinear(e1[k], e2[k], e3[k], h[k] + e1[k], h[k] + e2[k]) for k in range(5)]
        e2m = [at(em, c, j + 3 * r) for c in range(5)]
        e1, e3 = ([at(em, c, j + k * r) for c in range(5)] for k in (4, 2))
        h = [at(hm, c, j + 4 * r) for c in range(5)]
        e1, e2, e3, h = (project(u, *args) for u in (e1, e2m, e3, h))
        n = [n[k] + nonlinear(e1[k], e2[k], e3[k], e1[k] - h[k], e2[k] - h[k]) for k in range(5)]
        d = (c2 * ic) * (n[4] - n[0])
        s15 = n[0] + n[4]
        s = s15 + n[3]
        enthalpy = (1.0 / (GAMMA - 1.0)) * c2 + kin
        out = [
            s,
            vn * s + d,
            va * s + n[1],
            vb * s + n[2],
            enthalpy * s15 + vn * d + va * n[1] + vb * n[2] + kin * n[3],
        ]
        for c in range(5):
            linear = at(f6, c, j + 2 * r) + at(f6, c, j + 3 * r)
            linear = linear - at(ep, c, j + 2 * r) - at(em, c, j + 3 * r)
            put(flux, order[c], j, linear + out[c])
        return 0

    lax.fori_loop(0, (slots + 1) * r, face, 0)


def advance_kernel(cells, shape, cons, xh, yh, zh, zt, top, out, q, p, m, f6, ep, em, hp, hm, fx, fy, fz):
    lx, ly, lz = shape
    rows = lx * ly
    groups = rows // LANES
    blocks = 8 // groups
    inner = lz // blocks
    speeds = []
    for d in range(3):
        best = jnp.max(jnp.max(top[pl.ds(8 * d, 8), :], axis=0, keepdims=True), axis=1, keepdims=True)
        speeds.append(jnp.broadcast_to(best, (8, LANES)))
    step = COURANT / (speeds[0] * cells[0] + speeds[1] * cells[1] + speeds[2] * cells[2])
    work = (q, p, m, f6, ep, em, hp, hm)

    edge = 3 * ly
    q[:, pl.ds(0, edge), :] = xh[0]
    q[:, pl.ds(edge, rows), :] = cons[...]
    q[:, pl.ds(edge + rows, edge), :] = xh[1]
    flux_sweep(0, lx, ly // 8, 0.25 * speeds[0], *work, fx)

    edge = 3 * lx
    q[:, pl.ds(0, edge), :] = yh[0]
    for c in range(5):
        for y in range(ly):
            q[c, pl.ds(edge + y * lx, lx), :] = cons[c, pl.ds(y, lx, stride=ly), :]
    q[:, pl.ds(edge + rows, edge), :] = yh[1]
    flux_sweep(1, ly, lx // 8, 0.25 * speeds[1], *work, fy)

    size = inner * 8
    q[:, pl.ds(24, size), :] = zt[...]
    for c in range(5):
        for k in range(3):
            low, high = 8 * k, 24 + size + 8 * k
            q[c, low:low + groups, :] = zh[0, c, k]
            q[c, low + groups:low + 8, :] = zt[c, size - 24 + 8 * k:size - 16 + 8 * k - groups, :]
            q[c, high:high + 8 - groups, :] = zt[c, 8 * k + groups:8 * k + 8, :]
            q[c, high + 8 - groups:high + 8, :] = zh[1, c, k]
    flux_sweep(2, inner, 1, 0.25 * speeds[2], *work, fz)

    scale = [step * (cells[d] / 3.0) for d in range(3)]
    for c in range(5):
        def drop(j, _):
            here = pl.ds(pl.multiple_of(8 * j, 8), 8)
            fz[c, here, :] = scale[2] * (fz[c, here, :] - fz[c, pl.ds(pl.multiple_of(8 * j + 8, 8), 8), :])
            return 0

        lax.fori_loop(0, inner, drop, 0, unroll=4)
        for y in range(ly):
            for h in range(lx // 8):
                here = fy[c, pl.ds(y * lx + 8 * h, 8), :]
                there = fy[c, pl.ds((y + 1) * lx + 8 * h, 8), :]
                out[c, pl.ds(8 * h * ly + y, 8, stride=ly), :] = scale[1] * (here - there)
        for g in range(groups):
            parts = [fz[c, pl.ds(b * groups + g, inner, stride=8), :] for b in range(blocks)]
            turned = jnp.transpose(jnp.concatenate(parts, axis=0))
            for t in range(LANES // 8):
                at = g * LANES + 8 * t
                here = pl.ds(at, 8)
                along_x = scale[0] * (fx[c, here, :] - fx[c, pl.ds(at + ly, 8), :])
                out[c, here, :] = cons[c, here, :] + ((out[c, here, :] + along_x) + turned[8 * t:8 * t + 8])


def solution(mesh):
    sizes = [mesh.shape[axis] for axis in AXES]

    def per_device(conserved):
        _, lx, ly, lz = conserved.shape
        shape = (lx, ly, lz)
        cells = [float(n * s) for n, s in zip(shape, sizes)]
        rows = lx * ly
        groups = rows // LANES
        inner = lz * groups // 8
        assert lz == LANES and rows % LANES == 0 and 8 % groups == 0 and lx % 8 == 0 and ly % 8 == 0
        flat = conserved.reshape(5, rows, lz)
        vmem = pl.BlockSpec(memory_space=pltpu.VMEM)
        total = sum(s - 1 for s in sizes)
        f32 = jnp.float32
        xh, yh, zh, zt, top = pl.pallas_call(
            functools.partial(exchange_kernel, sizes, shape),
            name="exchange",
            out_shape=[
                jax.ShapeDtypeStruct((2, 5, 3 * ly, lz), f32),
                jax.ShapeDtypeStruct((2, 5, 3 * lx, lz), f32),
                jax.ShapeDtypeStruct((2, 5, 3, groups, LANES), f32),
                jax.ShapeDtypeStruct((5, inner * 8, LANES), f32),
                jax.ShapeDtypeStruct((24, LANES), f32),
            ],
            in_specs=[vmem],
            out_specs=[vmem] * 5,
            scratch_shapes=[
                pltpu.VMEM((2, 5, 3 * lx, lz), f32),
                pltpu.VMEM((2, 5, 3, groups, LANES), f32),
                pltpu.VMEM((3, 24, LANES), f32),
                pltpu.VMEM((total, 24, LANES), f32),
                pltpu.SemaphoreType.DMA((6,)),
                pltpu.SemaphoreType.DMA((6,)),
                pltpu.SemaphoreType.DMA((total,)),
                pltpu.SemaphoreType.DMA((total,)),
            ],
            compiler_params=pltpu.CompilerParams(collective_id=0, has_side_effects=True),
        )(flat)
        padded = max((lx + 6) * ly, (ly + 6) * lx, (inner + 6) * 8)
        work = pltpu.VMEM((5, padded, LANES), f32)
        out = pl.pallas_call(
            functools.partial(advance_kernel, cells, shape),
            name="advance",
            out_shape=jax.ShapeDtypeStruct((5, rows, lz), f32),
            in_specs=[vmem] * 6,
            out_specs=vmem,
            scratch_shapes=[work] * 8 + [
                pltpu.VMEM((5, (lx + 1) * ly, LANES), f32),
                pltpu.VMEM((5, (ly + 1) * lx, LANES), f32),
                pltpu.VMEM((5, (inner + 1) * 8, LANES), f32),
            ],
        )(flat, xh, yh, zh, zt, top)
        return out.reshape(conserved.shape)

    return jax.shard_map(
        per_device,
        mesh=mesh,
        in_specs=(P(None, "gx", "gy", "gz"),),
        out_specs=P(None, "gx", "gy", "gz"),
        check_vma=False,
    )
```

time: 101 us -> 33.7 us (0.33)
  other arithmetic: 41.7 us -> 0 us
  blocking collectives: 39.4 us -> 0 us
  Pallas kernels: 0 us -> 33.5 us
  starting transfers between devices: 10.5 us -> 0 us
  local copies, waits for them, and re-layouts: 7.14 us -> 0 us
  between operations: 2.3 us -> 0.01 us
    pmax x1 -> x0, blocking collectives: 39.4 us -> none  [per_device(): lax.pmax((local_x, local_y, local_z), ('gx', 'gy', 'gz'))]
    add x7 -> x0, other arithmetic: 34.1 us -> none  [the longest x6 33.7 us: multiply_rows(): accum = product_term if accum is None else accum + product_term]
    pallas_call x0 -> x2, Pallas kernels: none -> 33.5 us  [the longest x1 16.9 us: per_device(): pl.pallas_call(functools.partial(exchange_kernel, sizes, shape), name='ex...]
    ppermute x6 -> x0, starting transfers between devices: 10.5 us -> none  [the longest x3 8.13 us: padded(): after = lax.ppermute(first, axis, down)]
    mul x6 -> x0, other arithmetic: 5.07 us -> none  [the longest x3 2.74 us: face_divergence(): 0.5 * (flux + wave_speed * component)]
    slice x3 -> x0, local copies, waits for them, and re-layouts: 2.29 us -> none  [the longest x2 1.58 us: padded(): last = lax.slice_in_dim(shard, length - width, length, axis=dim)]
    ppermute x2 -> x0, local copies, waits for them, and re-layouts: 2 us -> none  [the longest x1 1.44 us: padded(): before = lax.ppermute(last, axis, up)]
    unnamed x7 -> x0, local copies, waits for them, and re-layouts: 1.58 us -> none
  transfers between devices with their start and end apart: 6 -> 0, of which waited for: 0 -> 0; matrix products, arithmetic and copies ran while one was open for 33% -> 0% of each run, Pallas kernels for 0% -> 0%
where the time goes in v1:
time: 33.7 us; the launch traced here: 33.6 us
  Pallas kernels  33.5 us (99%)
    pallas_call x1, Pallas kernels, per_device(): pl.pallas_call(functools.partial(exchange_kernel, sizes, shape), name='ex...  16.9 us
    pallas_call x1, Pallas kernels, per_device(): pl.pallas_call(functools.partial(advance_kernel, cells, shape), name='adv...  16.6 us

profile of v1, /device:TPU:0, one launch (start us, length us, event | category | flops | bytes accessed | tf_op | source)
XLA Modules:
  0.0 33.6 jit_solution(13128356471341323034)
XLA Ops:
  0.0 16.9 %exchange.1 = (f32[2,5,48,128]{3,2,1,0:T(8,128)}, f32[2,5,48,128]{3,2,1,0:T(8,128)}, f32[2,5,3,2,128]{4,3,2,1,0:T(2,128)}, f32[5,256,128]{2,1,0:T(8,128)}, f32[24,128]{1,0:T(8,128)}) custom-call(f32[5,256,128]{2,1,0:T(8,128)} %bitcast.2), custom_call_target="tpu_custom_call" | custom-call | tf_op jit(solution)/shard_map/exchange/pallas_call | solution.py:308
  16.9 16.6 %advance.1 = f32[5,256,128]{2,1,0:T(8,128)} custom-call(f32[5,256,128]{2,1,0:T(8,128)} %bitcast.3, f32[2,5,48,128]{3,2,1,0:T(8,128)} %get-tuple-element.10.xh, f32[2,5,48,128]{3,2,1,0:T(8,128)} %get-tuple-element.11.yh, f32[2,5,3,2,128]{4,3,2,1,0:T(2,128)} %get-tuple-element.12.zh, f32[5,256,128]{2,1,0:T(8,128)} %get-tuple-element.13.zt, ...), custom_call_target="tpu_custom_call" | custom-call | tf_op jit(solution)/shard_map/advance/pallas_call | solution.py:334

commit v2 on v1

v2 whole, which is shorter than its diff:
```python
import functools

import jax
import jax.numpy as jnp
from jax import lax
from jax.experimental import pallas as pl
from jax.experimental.pallas import tpu as pltpu
from jax.sharding import PartitionSpec as P

GAMMA = 1.4
EPS = 1e-06
COURANT = 0.4
K13 = 13.0 / 3.0
MESH = pl.DeviceIdType.MESH
AXES = ("gx", "gy", "gz")
ORDERS = ([0, 1, 2, 3, 4], [0, 2, 1, 3, 4], [0, 3, 1, 2, 4])
LANES = 128


def project(u, vn, va, vb, kin, b1h, ich):
    a = u[4] + kin * u[0] - vn * u[1] - va * u[2] - vb * u[3]
    a = b1h * a
    b = (vn * u[0] - u[1]) * ich
    return [a + b, u[2] - va * u[0], u[3] - vb * u[0], u[0] - (a + a), a - b]


def nonlinear(e1, e2, e3, f0, f1):
    f2 = e3 - (f1 + e2)
    q0 = 1.0 / ((K13 * (e1 * e1) + EPS) + f0 * f0)
    q1 = 1.0 / ((K13 * (e2 * e2) + EPS) + f1 * f1)
    q2 = 1.0 / ((K13 * (e3 * e3) + EPS) + f2 * f2)
    w0 = q0 * q0
    w2 = 3.0 * (q2 * q2)
    n0 = e1 - e2
    return (w0 * (n0 + n0) + w2 * (e2 - e3)) / (w0 + w2 + 6.0 * (q1 * q1))


def flux_sweep(direction, slots, lane_rows, quarter, q, p, m, f6, ep, em, hp, hm, flux):
    order = ORDERS[direction]

    def at(ref, c, j):
        return ref[c, pl.ds(pl.multiple_of(8 * j, 8), 8), :]

    def put(ref, c, j, value):
        ref[c, pl.ds(pl.multiple_of(8 * j, 8), 8), :] = value

    r = lane_rows

    def cell(j, _):
        s = [at(q, order[c], j) for c in range(5)]
        inv = 1.0 / s[0]
        vq = s[1] * (0.25 * inv)
        pq = 0.25 * (GAMMA - 1.0) * (s[4] - (0.5 * inv) * (s[1] * s[1] + s[2] * s[2] + s[3] * s[3]))
        f = [0.25 * s[1], s[1] * vq + pq, s[2] * vq, s[3] * vq, s[4] * vq + 4.0 * (pq * vq)]
        for c in range(5):
            sq = quarter * s[c]
            put(p, c, j, f[c] + sq)
            put(m, c, j, f[c] - sq)
            put(f6, c, j, 6.0 * f[c])
        return 0

    lax.fori_loop(0, (slots + 6) * r, cell, 0, unroll=2)

    def differ(i, _):
        j = i + r
        for c in range(5):
            for src, e, h in ((p, ep, hp), (m, em, hm)):
                low, mid, high = at(src, c, j - r), at(src, c, j), at(src, c, j + r)
                below = mid - low
                put(e, c, j, (high - mid) - below)
                put(h, c, j, below + below)
        return 0

    lax.fori_loop(0, (slots + 4) * r, differ, 0, unroll=2)

    def face(j, _):
        mean = [at(q, order[c], j + 2 * r) + at(q, order[c], j + 3 * r) for c in range(5)]
        inv = 1.0 / mean[0]
        vn, va, vb = mean[1] * inv, mean[2] * inv, mean[3] * inv
        kin = 0.5 * (vn * vn + va * va + vb * vb)
        c2 = GAMMA * (GAMMA - 1.0) * (mean[4] * inv - kin)
        ic = lax.rsqrt(c2)
        b1h = (0.5 * (GAMMA - 1.0)) * (ic * ic)
        ich = 0.5 * ic
        args = (vn, va, vb, kin, b1h, ich)
        e2p = [at(ep, c, j + 2 * r) for c in range(5)]
        e1, e3 = ([at(ep, c, j + k * r) for c in range(5)] for k in (1, 3))
        h = [at(hp, c, j + 2 * r) for c in range(5)]
        e1, e2, e3, h = (project(u, *args) for u in (e1, e2p, e3, h))
        n = [nonlinear(e1[k], e2[k], e3[k], h[k] + e1[k], h[k] + e2[k]) for k in range(5)]
        e2m = [at(em, c, j + 3 * r) for c in range(5)]
        e1, e3 = ([at(em, c, j + k * r) for c in range(5)] for k in (4, 2))
        h = [at(hm, c, j + 4 * r) for c in range(5)]
        e1, e2, e3, h = (project(u, *args) for u in (e1, e2m, e3, h))
        n = [n[k] + nonlinear(e1[k], e2[k], e3[k], e1[k] - h[k], e2[k] - h[k]) for k in range(5)]
        d = (c2 * ic) * (n[4] - n[0])
        s15 = n[0] + n[4]
        s = s15 + n[3]
        enthalpy = (1.0 / (GAMMA - 1.0)) * c2 + kin
        out = [
            s,
            vn * s + d,
            va * s + n[1],
            vb * s + n[2],
            enthalpy * s15 + vn * d + va * n[1] + vb * n[2] + kin * n[3],
        ]
        for c in range(5):
            linear = at(f6, c, j + 2 * r) + at(f6, c, j + 3 * r)
            linear = linear - at(ep, c, j + 2 * r) - at(em, c, j + 3 * r)
            put(flux, order[c], j, linear + out[c])
        return 0

    lax.fori_loop(0, (slots + 1) * r, face, 0)


def section_kernel(
    sizes, cells, shape, cons_hbm, out_hbm, cons, out, qx, qy, qz, xh, yh, zh, ysend, zsend, mine, theirs,
    p, m, f6, ep, em, hp, hm, fx, fy, fz, halo_send, halo_recv, max_send, max_recv, load_sem, store_sem,
):
    lx, ly, lz = shape
    rows = lx * ly
    groups = rows // LANES
    blocks = 8 // groups
    inner = lz // blocks
    load = pltpu.make_async_copy(cons_hbm, cons, load_sem)
    load.start()
    peers = []
    for axis, size in zip(AXES, sizes):
        me = lax.axis_index(axis)
        peers.append([{axis: lax.rem(me + k, size)} for k in range(1, size)])
    barrier = pltpu.get_barrier_semaphore()
    count = 0
    for axis_peers in peers:
        for peer in axis_peers:
            pl.semaphore_signal(barrier, inc=1, device_id=peer, device_id_type=MESH)
            count += 1
    load.wait()

    best = [None] * 3
    for j in range(rows // 8):
        q = [cons[c, pl.ds(8 * j, 8), :] for c in range(5)]
        inv = 1.0 / q[0]
        vel = [q[d] * inv for d in (1, 2, 3)]
        kinetic = 0.5 * (vel[0] * vel[0] + vel[1] * vel[1] + vel[2] * vel[2])
        sound = jnp.sqrt((GAMMA * (GAMMA - 1.0)) * (q[4] * inv - kinetic))
        for d in range(3):
            value = jnp.abs(vel[d]) + sound
            best[d] = value if best[d] is None else jnp.maximum(best[d], value)
    for d in range(3):
        mine[0, pl.ds(d, 1), :] = jnp.max(best[d], axis=0, keepdims=True)
    mine[0, pl.ds(3, 5), :] = jnp.zeros((5, LANES), jnp.float32)

    for c in range(5):
        for k in range(3):
            ysend[0, c, pl.ds(k * lx, lx), :] = cons[c, pl.ds(ly - 3 + k, lx, stride=ly), :]
            ysend[1, c, pl.ds(k * lx, lx), :] = cons[c, pl.ds(k, lx, stride=ly), :]

    def halo(slot, src, dst, axis, size, up):
        me = lax.axis_index(axis)
        target = lax.rem(me + (1 if up else size - 1), size)
        return pltpu.make_async_remote_copy(
            src_ref=src, dst_ref=dst, send_sem=halo_send.at[slot], recv_sem=halo_recv.at[slot],
            device_id={axis: target}, device_id_type=MESH,
        )

    def spread(place, stage):
        size = sizes[stage]
        copies = []
        for k in range(size - 1):
            slot = sum(s - 1 for s in sizes[:stage]) + k
            copy = pltpu.make_async_remote_copy(
                src_ref=mine.at[place], dst_ref=theirs.at[slot],
                send_sem=max_send.at[slot], recv_sem=max_recv.at[slot],
                device_id=peers[stage][k], device_id_type=MESH,
            )
            copy.start()
            copies.append((slot, copy))
        return copies

    def gather(place, copies):
        value = mine[place]
        for slot, copy in copies:
            copy.wait_recv()
            value = jnp.maximum(value, theirs[slot])
        return value

    pl.semaphore_wait(barrier, count)
    first = spread(0, 0)
    edge = 3 * ly
    along_x = [
        halo(0, cons.at[:, pl.ds(rows - edge, edge), :], xh.at[0], "gx", sizes[0], True),
        halo(1, cons.at[:, pl.ds(0, edge), :], xh.at[1], "gx", sizes[0], False),
    ]
    along_y = [
        halo(2, ysend.at[0], yh.at[0], "gy", sizes[1], True),
        halo(3, ysend.at[1], yh.at[1], "gy", sizes[1], False),
    ]
    along_z = [
        halo(4, zsend.at[0], zh.at[0], "gz", sizes[2], True),
        halo(5, zsend.at[1], zh.at[1], "gz", sizes[2], False),
    ]
    for copy in along_y + along_x:
        copy.start()

    for c in range(5):
        for g in range(groups):
            turned = jnp.transpose(cons[c, pl.ds(g * LANES, LANES), :])
            for b in range(blocks):
                qz[c, pl.ds(24 + b * groups + g, inner, stride=8), :] = turned[b * inner:(b + 1) * inner]
            for k in range(3):
                zsend[0, c, k, g:g + 1, :] = turned[lz - 3 + k:lz - 2 + k]
                zsend[1, c, k, g:g + 1, :] = turned[k:k + 1]

    mine[1] = gather(0, first)
    second = spread(1, 2)
    for copy in along_z:
        copy.start()

    y_edge = 3 * lx
    for c in range(5):
        for y in range(ly):
            qy[c, pl.ds(y_edge + y * lx, lx), :] = cons[c, pl.ds(y, lx, stride=ly), :]

    mine[2] = gather(1, second)
    third = spread(2, 1)
    for copy in along_y:
        copy.wait()
    qy[:, pl.ds(0, y_edge), :] = yh[0]
    qy[:, pl.ds(y_edge + rows, y_edge), :] = yh[1]
    qx[:, pl.ds(edge, rows), :] = cons[...]
    top = gather(2, third)
    for _, copy in first + second + third:
        copy.wait_send()

    speeds = []
    for d in range(3):
        largest = jnp.max(top[d:d + 1], axis=1, keepdims=True)
        speeds.append(jnp.broadcast_to(largest, (8, LANES)))
    step = COURANT / (speeds[0] * cells[0] + speeds[1] * cells[1] + speeds[2] * cells[2])
    work = (p, m, f6, ep, em, hp, hm)

    flux_sweep(1, ly, lx // 8, 0.25 * speeds[1], qy, *work, fy)

    for copy in along_z:
        copy.wait()
    size = inner * 8
    for c in range(5):
        for k in range(3):
            low, high = 8 * k, 24 + size + 8 * k
            qz[c, low:low + groups, :] = zh[0, c, k]
            qz[c, low + groups:low + 8, :] = qz[c, size + 8 * k:size + 8 + 8 * k - groups, :]
            qz[c, high:high + 8 - groups, :] = qz[c, 24 + 8 * k + groups:32 + 8 * k, :]
            qz[c, high + 8 - groups:high + 8, :] = zh[1, c, k]
    flux_sweep(2, inner, 1, 0.25 * speeds[2], qz, *work, fz)

    for copy in along_x:
        copy.wait()
    qx[:, pl.ds(0, edge), :] = xh[0]
    qx[:, pl.ds(edge + rows, edge), :] = xh[1]
    flux_sweep(0, lx, ly // 8, 0.25 * speeds[0], qx, *work, fx)

    scale = [step * (cells[d] / 3.0) for d in range(3)]
    stores = []
    for c in range(5):
        def drop(j, _):
            here = pl.ds(pl.multiple_of(8 * j, 8), 8)
            fz[c, here, :] = scale[2] * (fz[c, here, :] - fz[c, pl.ds(pl.multiple_of(8 * j + 8, 8), 8), :])
            return 0

        lax.fori_loop(0, inner, drop, 0, unroll=8)
        for y in range(ly):
            for h in range(lx // 8):
                here = fy[c, pl.ds(y * lx + 8 * h, 8), :]
                there = fy[c, pl.ds((y + 1) * lx + 8 * h, 8), :]
                out[c, pl.ds(8 * h * ly + y, 8, stride=ly), :] = scale[1] * (here - there)
        for g in range(groups):
            parts = [fz[c, pl.ds(b * groups + g, inner, stride=8), :] for b in range(blocks)]
            turned = jnp.transpose(jnp.concatenate(parts, axis=0))
            for t in range(LANES // 8):
                at = g * LANES + 8 * t
                here = pl.ds(at, 8)
                change = scale[0] * (fx[c, here, :] - fx[c, pl.ds(at + ly, 8), :])
                out[c, here, :] = cons[c, here, :] + ((out[c, here, :] + change) + turned[8 * t:8 * t + 8])
        stores.append(pltpu.make_async_copy(out.at[c], out_hbm.at[c], store_sem.at[c]))
        if c > 0:
            stores[c - 1].start()
    stores[-1].start()
    for store in stores:
        store.wait()


def solution(mesh):
    sizes = [mesh.shape[axis] for axis in AXES]

    def per_device(conserved):
        _, lx, ly, lz = conserved.shape
        shape = (lx, ly, lz)
        cells = [float(n * s) for n, s in zip(shape, sizes)]
        rows = lx * ly
        groups = rows // LANES
        inner = lz * groups // 8
        assert lz == LANES and rows % LANES == 0 and 8 % groups == 0 and lx % 8 == 0 and ly % 8 == 0
        total = sum(s - 1 for s in sizes)

        def vmem(*dims):
            return pltpu.VMEM(dims, jnp.float32)

        padded = max((lx + 6) * ly, (ly + 6) * lx, (inner + 6) * 8)
        out = pl.pallas_call(
            functools.partial(section_kernel, sizes, cells, shape),
            name="section",
            out_shape=jax.ShapeDtypeStruct((5, rows, lz), jnp.float32),
            in_specs=[pl.BlockSpec(memory_space=pl.ANY)],
            out_specs=pl.BlockSpec(memory_space=pl.ANY),
            scratch_shapes=[
                vmem(5, rows, lz),
                vmem(5, rows, lz),
                vmem(5, padded, LANES),
                vmem(5, padded, LANES),
                vmem(5, padded, LANES),
                vmem(2, 5, 3 * ly, lz),
                vmem(2, 5, 3 * lx, lz),
                vmem(2, 5, 3, groups, LANES),
                vmem(2, 5, 3 * lx, lz),
                vmem(2, 5, 3, groups, LANES),
                vmem(3, 8, LANES),
                vmem(total, 8, LANES),
            ] + [vmem(5, padded, LANES)] * 7 + [
                vmem(5, (lx + 1) * ly, LANES),
                vmem(5, (ly + 1) * lx, LANES),
                vmem(5, (inner + 1) * 8, LANES),
                pltpu.SemaphoreType.DMA((6,)),
                pltpu.SemaphoreType.DMA((6,)),
                pltpu.SemaphoreType.DMA((total,)),
                pltpu.SemaphoreType.DMA((total,)),
                pltpu.SemaphoreType.DMA,
                pltpu.SemaphoreType.DMA((5,)),
            ],
            compiler_params=pltpu.CompilerParams(collective_id=0, has_side_effects=True),
        )(conserved.reshape(5, rows, lz))
        return out.reshape(conserved.shape)

    return jax.shard_map(
        per_device,
        mesh=mesh,
        in_specs=(P(None, "gx", "gy", "gz"),),
        out_specs=P(None, "gx", "gy", "gz"),
        check_vma=False,
    )
```

time: 33.7 us -> 30 us (0.89)
  Pallas kernels: 33.5 us -> 27.8 us
  local copies, waits for them, and re-layouts: 0 us -> 1.99 us
    pallas_call x2 -> x1, Pallas kernels: 33.5 us -> 27.8 us  [per_device(): pl.pallas_call(functools.partial(section_kernel, sizes, cells, shape), na...]
    unnamed x0 -> x1, local copies, waits for them, and re-layouts: none -> 1.99 us
where the time goes in v2:
time: 30 us; the launch traced here: 29.8 us
  Pallas kernels  27.8 us (93%)
  local copies, waits for them, and re-layouts  1.99 us (7%)
    pallas_call x1, Pallas kernels, per_device(): pl.pallas_call(functools.partial(section_kernel, sizes, cells, shape), na...  27.8 us
    unnamed x1, local copies, waits for them, and re-layouts  1.99 us

profile of v2, /device:TPU:0, one launch (start us, length us, event | category | flops | bytes accessed | tf_op | source)
XLA Modules:
  0.0 29.8 jit_solution(7380660098409933173)
XLA Ops:
  0.0 27.8 %section.1 = f32[5,256,128]{2,1,0:T(8,128)} custom-call(f32[5,256,128]{2,1,0:T(8,128)} %bitcast.3), custom_call_target="tpu_custom_call" | custom-call | tf_op jit(solution)/shard_map/section/pallas_call | solution.py:309
  27.9 2.0 %copy.3 = f32[5,16,16,128]{3,2,1,0:T(8,128)} copy(f32[5,16,16,128]{3,2,1,0:T(8,128)} %bitcast.2) | data formatting | bytes 1310720
